TPU v7x, 32 devices: a whole 2x2x4 slice. The times are simulated.
32 devices in a mesh: kx: 4 (over z), ky: 4 (over x, core), kz: 2 (over y).
Axes of the slice: x: 2, y: 2, z: 4, core: 2. Of those that a mesh axis runs over, the one named last changes fastest.
Arguments:
- offsets: int32 [12, 3], replicated, may hold values from -1 to 1, as said below
- gauge: float32 [2, 4, 4, 4, 256, 256], P(None, 'kx', 'ky', 'kz'), may hold values from -1 to 1, as said below
- intersections: bfloat16 [12, 2, 4, 4, 4, 256, 256], P(None, None, 'kx', 'ky', 'kz'), may hold values from -1 to 1
Outputs:
- new_gauge: float32 [2, 4, 4, 4, 256, 256], P(None, 'kx', 'ky', 'kz')
- centres: float32 [3, 256], replicated
- spread: float32 [], replicated
Inputs may be any that keep to these rules, and one draw needn't show every extreme that they name: `offsets`: the 12 rows are the twelve distinct vectors with two entries of magnitude one and one entry zero, each once. `gauge`: every 256 x 256 complex matrix of it is unitary to float32 rounding.
All inputs are finite; a program needn't handle non-finite values.
Results may differ from a plain program's by a relative error of at most 0.0068.
Values may be sent and summed in bfloat16 or wider, within the bound.
A program may use at most 192 MiB of HBM per device.

v0:
```python
import functools
import math

import jax
import jax.numpy as jnp
import numpy as np
from jax import lax
from jax.experimental import pallas as pl
from jax.experimental.pallas import tpu as pltpu
from jax.sharding import PartitionSpec as P

TERMS = 12
MAGNITUDE_FLOOR = 0.25
DESCENT_STEP = 2.0
MESH = pl.DeviceIdType.MESH
AXES = ("kx", "ky", "kz")

DIRECTIONS = (
    [(sx, 0, sz) for sx in (-1, 1) for sz in (-1, 1)]
    + [(0, sy, sz) for sy in (-1, 1) for sz in (-1, 1)]
    + [(sx, sy, 0) for sx in (-1, 1) for sy in (-1, 1)]
)


def at(ref, *index):
    return ref.at[index]


def atan2(y, x):
    negative_y = (y < 0) | ((y == 0) & (1.0 / y < 0))
    negative_x = (x < 0) | ((x == 0) & (1.0 / x < 0))
    abs_y, abs_x = jnp.abs(y), jnp.abs(x)
    high, low = jnp.maximum(abs_y, abs_x), jnp.minimum(abs_y, abs_x)
    ratio = jnp.where(high == 0, 0.0, low / jnp.where(high == 0, 1.0, high))
    shifted = ratio > 0.4142135623730950
    t = jnp.where(shifted, (ratio - 1.0) / (ratio + 1.0), ratio)
    z = t * t
    poly = ((8.05374449538e-2 * z - 1.38776856032e-1) * z + 1.99777106478e-1) * z - 3.33329491539e-1
    angle = poly * z * t + t
    angle = jnp.where(shifted, angle + math.pi / 4, angle)
    angle = jnp.where(abs_y > abs_x, math.pi / 2 - angle, angle)
    angle = jnp.where(negative_x, math.pi - angle, angle)
    return jnp.where(negative_y, -angle, angle)


def gather_kernel(
    sizes,
    total_k,
    perm_ref,
    coef_ref,
    own_hbm,
    inter_hbm,
    z_ref,
    centres_ref,
    spread_ref,
    own_ref,
    inter_ref,
    basis_ref,
    left_ref,
    near_ref,
    end_ref,
    m_ref,
    dr_ref,
    di_ref,
    parts_ref,
    sums_x,
    sums_y,
    sums_z,
    local_sem,
    send_sem,
    recv_sem,
    part_send,
    part_recv,
):
    depth = own_ref.shape[0]
    rows = own_ref.shape[1]
    n = rows // 2
    place = [lax.axis_index(axis) for axis in AXES]

    def step(axis, by):
        return {AXES[axis]: lax.rem(place[axis] + by + sizes[axis], sizes[axis])}

    own_copy = pltpu.make_async_copy(own_hbm, own_ref, local_sem.at[0])
    inter_copy = pltpu.make_async_copy(inter_hbm, inter_ref, local_sem.at[1])
    own_copy.start()
    inter_copy.start()

    barrier = pltpu.get_barrier_semaphore()
    partners = 0
    for axis in range(3):
        for by in range(1, sizes[axis]):
            pl.semaphore_signal(barrier, inc=1, device_id=step(axis, by), device_id_type=MESH)
            partners += 1
    pl.semaphore_wait(barrier, partners)

    counter = [0]
    sent = []

    def send(source, target, device):
        index = counter[0]
        counter[0] += 1
        copy = pltpu.make_async_remote_copy(
            src_ref=source,
            dst_ref=target,
            send_sem=send_sem.at[index],
            recv_sem=recv_sem.at[index],
            device_id=device,
            device_id_type=MESH,
        )
        copy.start()
        sent.append(copy)
        return copy

    signs = (-1, 1)
    along_x, along_y, corner, rim = {}, {}, {}, {}
    for j in range(depth):
        for s, sign in enumerate(signs):
            along_x[s, j] = send(own_hbm.at[j], near_ref.at[s, 1 + j], step(0, -sign))
    end = send(own_hbm.at[0], end_ref, step(2, -1))
    for j in reversed(range(depth)):
        for s, sign in enumerate(signs):
            along_y[s, j] = send(own_hbm.at[j], near_ref.at[2 + s, 1 + j], step(1, -sign))

    own_copy.wait()

    def make_basis(j, carry):
        u = own_ref[j].astype(jnp.float32)
        real = u[:n].T
        imag = u[n:].T
        basis_ref[j, :n, :n] = real.astype(jnp.bfloat16)
        basis_ref[j, :n, n:] = imag.astype(jnp.bfloat16)
        basis_ref[j, n:, :n] = (-imag).astype(jnp.bfloat16)
        basis_ref[j, n:, n:] = real.astype(jnp.bfloat16)
        return carry

    lax.fori_loop(0, depth, make_basis, 0)
    inter_copy.wait()

    def make_left(q, carry):
        j = lax.rem(q, depth)
        b = perm_ref[q // depth]
        right = jnp.concatenate([inter_ref[b, 0, j], inter_ref[b, 1, j]], axis=0)
        left = jnp.dot(basis_ref[j], right, preferred_element_type=jnp.float32)
        left_ref[q] = left.astype(jnp.bfloat16)
        return carry

    lax.fori_loop(0, len(DIRECTIONS) * depth, make_left, 0)

    row_id = lax.broadcasted_iota(jnp.int32, (n, n), 0)
    col_id = lax.broadcasted_iota(jnp.int32, (n, n), 1)

    def multiply(direction, j, column, slot):
        q = direction * depth + j
        left = left_ref[q]
        real, imag = left[:n], left[n:]
        full = jnp.concatenate(
            [jnp.concatenate([real, -imag], axis=1), jnp.concatenate([imag, real], axis=1)], axis=0
        )
        m = jnp.dot(full, near_ref[column, slot], preferred_element_type=jnp.float32)
        m_ref[q] = m
        diagonal = row_id == col_id
        dr_ref[pl.ds(q, 1), :] = jnp.sum(jnp.where(diagonal, m[:n], 0.0), axis=0, keepdims=True)
        di_ref[pl.ds(q, 1), :] = jnp.sum(jnp.where(diagonal, m[n:], 0.0), axis=0, keepdims=True)

    def inner_edges(first):
        count = 2 * (depth - 1)

        def body(i, carry):
            s = i // count
            r = lax.rem(i, count)
            up = r // (depth - 1)
            j = lax.rem(r, depth - 1) + 1 - up
            column = first + s
            multiply(2 * column + up, j, column, 1 + j + 2 * up - 1)
            return carry

        if count:
            lax.fori_loop(0, 2 * count, body, 0)

    def outer_edges(first, up):
        j = depth - 1 if up else 0

        def body(s, carry):
            column = first + s
            multiply(2 * column + up, j, column, 1 + j + 2 * up - 1)
            return carry

        lax.fori_loop(0, 2, body, 0)

    for j in reversed(range(depth)):
        for s in range(2):
            along_y[s, j].wait_recv()
            if j == depth - 1:
                rim[1, s, 0] = send(
                    near_ref.at[2 + s, depth], near_ref.at[2 + s, 0], step(2, 1)
                )
    end.wait_recv()
    for s, sign in enumerate(signs):
        rim[1, s, 1] = send(end_ref, near_ref.at[2 + s, depth + 1], step(1, -sign))
    inner_edges(2)

    for j in range(depth):
        for s in range(2):
            along_x[s, j].wait_recv()
            source = near_ref.at[s, 1 + j]
            for other, sign in enumerate(signs):
                corner[s, other, j] = send(
                    source, near_ref.at[4 + 2 * s + other, 1 + j], step(1, -sign)
                )
            if j == depth - 1:
                rim[0, s, 0] = send(source, near_ref.at[s, 0], step(2, 1))
            if j == 0:
                rim[0, s, 1] = send(source, near_ref.at[s, depth + 1], step(2, -1))
    inner_edges(0)

    for up in range(2):
        for s in range(2):
            rim[1, s, up].wait_recv()
        outer_edges(2, up)

    for j in range(depth):
        for s in range(2):
            for other in range(2):
                corner[s, other, j].wait_recv()

        def corners(c, carry, j=j):
            multiply(8 + c, j, 4 + c, 1 + j)
            return carry

        lax.fori_loop(0, 4, corners, 0)

    for up in (1, 0):
        for s in range(2):
            rim[0, s, up].wait_recv()
        outer_edges(0, up)

    dr, di = dr_ref[...], di_ref[...]
    phase = atan2(di, dr)
    squared = dr * dr + di * di
    coef = coef_ref[...]
    weight = coef[:, 0:1]
    weighted = weight * phase
    parts = [
        jnp.sum(coef[:, 1 + a : 2 + a] * weighted, axis=0, keepdims=True) for a in range(3)
    ]
    parts.append(
        jnp.sum(weight * (1.0 - squared + phase * phase), axis=0, keepdims=True)
    )
    parts.append(jnp.zeros((4, n), jnp.float32))
    value = jnp.concatenate(parts, axis=0)
    index = 0
    for axis, slots in enumerate((sums_z, sums_y, sums_x)):
        axis = 2 - axis
        size = sizes[axis]
        me = place[axis]
        parts_ref[axis] = value
        slots[me] = value
        arrivals = []
        for by in range(1, size):
            copy = pltpu.make_async_remote_copy(
                src_ref=parts_ref.at[axis],
                dst_ref=slots.at[me],
                send_sem=part_send.at[index],
                recv_sem=part_recv.at[index],
                device_id=step(axis, by),
                device_id_type=MESH,
            )
            copy.start()
            sent.append(copy)
            source = lax.rem(me + size - by, size)
            arrivals.append(
                pltpu.make_async_remote_copy(
                    src_ref=parts_ref.at[axis],
                    dst_ref=slots.at[source],
                    send_sem=part_send.at[index],
                    recv_sem=part_recv.at[index],
                    device_id=step(axis, by),
                    device_id_type=MESH,
                )
            )
            index += 1
        for copy in arrivals:
            copy.wait_recv()
        value = slots[0]
        for other in range(1, size):
            value = value + slots[other]

    centres = -value[0:3] / total_k
    centres_ref[...] = centres
    per_band = value[3:4] / total_k - jnp.sum(centres * centres, axis=0, keepdims=True)
    spread_ref[...] = jnp.sum(per_band, axis=1, keepdims=True)

    angle = phase
    for a in range(3):
        angle = angle + coef[:, 1 + a : 2 + a] * centres[a : a + 1]
    angle = angle / jnp.maximum(squared, MAGNITUDE_FLOOR)
    dr_ref[...] = weight * (dr + di * angle)
    di_ref[...] = weight * (dr * angle - di)

    strip = 32

    def combine(i, carry):
        j = i // (n // strip)
        start = pl.multiple_of(lax.rem(i, n // strip) * strip, strip)
        real = jnp.zeros((strip, n), jnp.float32)
        imag = jnp.zeros((strip, n), jnp.float32)
        for d in range(len(DIRECTIONS)):
            q = d * depth + j
            cr = dr_ref[pl.ds(q, 1), :]
            ci = di_ref[pl.ds(q, 1), :]
            mr = m_ref[q, pl.ds(start, strip), :]
            mi = m_ref[q, pl.ds(n + start, strip), :]
            real = real + (mr * cr - mi * ci)
            imag = imag + (mr * ci + mi * cr)
        z_ref[j, 0, pl.ds(start, strip), :] = real
        z_ref[j, 1, pl.ds(start, strip), :] = imag
        return carry

    lax.fori_loop(0, depth * (n // strip), combine, 0)

    for copy in sent:
        copy.wait_send()


def split(value):
    high = value.astype(jnp.bfloat16)
    return high, (value - high.astype(jnp.float32)).astype(jnp.bfloat16)


def product(left, right):
    lr, li = split(left[0]), split(left[1])
    rr, ri = split(right[0]), split(right[1])
    n = left[0].shape[0]

    def full(part):
        real, imag = lr[part], li[part]
        return jnp.concatenate(
            [jnp.concatenate([real, -imag], axis=1), jnp.concatenate([imag, real], axis=1)], axis=0
        )

    high, low = full(0), full(1)
    r_high = jnp.concatenate([rr[0], ri[0]], axis=0)
    r_low = jnp.concatenate([rr[1], ri[1]], axis=0)
    out = jnp.dot(high, r_high, preferred_element_type=jnp.float32)
    out = out + (
        jnp.dot(high, r_low, preferred_element_type=jnp.float32)
        + jnp.dot(low, r_high, preferred_element_type=jnp.float32)
    )
    return out[:n], out[n:]


def exponential_kernel(z_ref, gauge_ref, out_ref):
    zr, zi = z_ref[0, 0], z_ref[0, 1]
    n = zr.shape[0]
    scale = 0.5 * DESCENT_STEP * 4.0
    x1 = (scale * (zr - zr.T), scale * (zi + zi.T))
    diagonal = lax.broadcasted_iota(jnp.int32, (n, n), 0) == lax.broadcasted_iota(
        jnp.int32, (n, n), 1
    )
    x2 = product(x1, x1)
    x3 = product(x1, x2)
    x4 = product(x2, x2)
    inverse = [1.0 / math.factorial(k) for k in range(TERMS + 1)]

    def group(first, powers):
        real = jnp.where(diagonal, inverse[first], 0.0)
        imag = jnp.zeros((n, n), jnp.float32)
        for k, power in enumerate(powers):
            real = real + inverse[first + 1 + k] * power[0]
            imag = imag + inverse[first + 1 + k] * power[1]
        return real, imag

    total = group(8, (x1, x2, x3, x4))
    for first in (4, 0):
        scaled = product(x4, total)
        base = group(first, (x1, x2, x3))
        total = (base[0] + scaled[0], base[1] + scaled[1])
    new = product((gauge_ref[0, 0], gauge_ref[1, 0]), total)
    out_ref[0, 0] = new[0]
    out_ref[1, 0] = new[1]


def per_device(sizes, offsets, gauge, intersections):
    depth, n = gauge.shape[3], gauge.shape[4]
    counts = (sizes[0], sizes[1], sizes[2] * depth)
    total_k = counts[0] * counts[1] * counts[2]
    table = np.array(DIRECTIONS, np.float64)
    bvec = table * (2.0 * math.pi / np.array(counts, np.float64))
    weight = 1.0 / (4.0 * np.sum(bvec * bvec, axis=1))
    queue = len(DIRECTIONS) * depth
    coef = np.zeros((queue, 128), np.float32)
    coef[:, 0] = np.repeat(weight, depth)
    coef[:, 1:4] = np.repeat(bvec, depth, axis=0)
    canonical = jnp.array(DIRECTIONS, jnp.int32)
    same = jnp.all(canonical[:, None, :] == offsets[None, :, :], axis=2)
    order = lax.broadcasted_iota(jnp.int32, same.shape, 1)
    perm = jnp.sum(jnp.where(same, order, 0), axis=1)

    flat = gauge.reshape(2, depth, n, n)
    own = jnp.swapaxes(flat.astype(jnp.bfloat16), 0, 1).reshape(depth, 2 * n, n)
    inter = intersections.reshape(len(DIRECTIONS), 2, depth, n, n)
    copies = 5 * depth + 1 + 4 * depth + 8
    bf16, f32 = jnp.bfloat16, jnp.float32
    partners = sum(size - 1 for size in sizes)
    z, centres, spread = pl.pallas_call(
        functools.partial(gather_kernel, sizes, float(total_k)),
        out_shape=(
            jax.ShapeDtypeStruct((depth, 2, n, n), f32),
            jax.ShapeDtypeStruct((3, n), f32),
            jax.ShapeDtypeStruct((1, 1), f32),
        ),
        in_specs=[
            pl.BlockSpec(memory_space=pltpu.SMEM),
            pl.BlockSpec(memory_space=pltpu.VMEM),
            pl.BlockSpec(memory_space=pl.ANY),
            pl.BlockSpec(memory_space=pl.ANY),
        ],
        out_specs=(
            pl.BlockSpec(memory_space=pltpu.VMEM),
            pl.BlockSpec(memory_space=pltpu.VMEM),
            pl.BlockSpec(memory_space=pltpu.VMEM),
        ),
        scratch_shapes=[
            pltpu.VMEM((depth, 2 * n, n), bf16),
            pltpu.VMEM(inter.shape, bf16),
            pltpu.VMEM((depth, 2 * n, 2 * n), bf16),
            pltpu.VMEM((queue, 2 * n, n), bf16),
            pltpu.VMEM((8, depth + 2, 2 * n, n), bf16),
            pltpu.VMEM((2 * n, n), bf16),
            pltpu.VMEM((queue, 2 * n, n), f32),
            pltpu.VMEM((queue, n), f32),
            pltpu.VMEM((queue, n), f32),
            pltpu.VMEM((3, 8, n), f32),
            pltpu.VMEM((sizes[0], 8, n), f32),
            pltpu.VMEM((sizes[1], 8, n), f32),
            pltpu.VMEM((sizes[2], 8, n), f32),
            pltpu.SemaphoreType.DMA((2,)),
            pltpu.SemaphoreType.DMA((copies,)),
            pltpu.SemaphoreType.DMA((copies,)),
            pltpu.SemaphoreType.DMA((partners,)),
            pltpu.SemaphoreType.DMA((partners,)),
        ],
        compiler_params=pltpu.CompilerParams(
            collective_id=0, has_side_effects=True, vmem_limit_bytes=58 * 1024 * 1024
        ),
        name="gather",
    )(perm, jnp.asarray(coef), own, inter)

    updated = pl.pallas_call(
        exponential_kernel,
        grid=(depth,),
        out_shape=jax.ShapeDtypeStruct((2, depth, n, n), f32),
        in_specs=[
            pl.BlockSpec((1, 2, n, n), lambda j: (j, 0, 0, 0)),
            pl.BlockSpec((2, 1, n, n), lambda j: (0, j, 0, 0)),
        ],
        out_specs=pl.BlockSpec((2, 1, n, n), lambda j: (0, j, 0, 0)),
        compiler_params=pltpu.CompilerParams(vmem_limit_bytes=48 * 1024 * 1024),
        name="exponential",
    )(z, flat)
    return updated.reshape(2, 1, 1, depth, n, n), centres, spread.reshape(())


def solution(mesh):
    sizes = tuple(mesh.shape[axis] for axis in AXES)
    return jax.shard_map(
        functools.partial(per_device, sizes),
        mesh=mesh,
        in_specs=(
            P(),
            P(None, "kx", "ky", "kz", None, None),
            P(None, None, "kx", "ky", "kz", None, None),
        ),
        out_specs=(P(None, "kx", "ky", "kz", None, None), P(), P()),
        check_vma=False,
    )
```

profile of v0, /device:TPU:0, one launch (start us, length us, event | category | flops | bytes accessed | tf_op | source)
XLA Modules:
  0.0 83.5 jit_solution(8574533108952665089)
XLA Ops:
  0.6 0.0 copy-start
  0.6 0.9 %compare_reduce_fusion = pred[12,12]{1,0:T(8,128)(4,1)S(1)} fusion(s32[12,3]{0,1:T(4,128)} %param.5, s32[12,3]{0,1:T(4,128)} %constant.8.clone), kind=kLoop, calls=%fused_computation.1 | loop fusion | flops 720 | bytes 432 | tf_op jit(solution)/shard_map/reduce_and | solution.py:395
  1.5 0.6 select_reduce_fusion.perm_ref
  2.1 1.3 %convert_bitcast_fusion = bf16[2,2,256,256]{3,2,0,1:T(8,128)(2,1)S(1)} fusion(f32[2,1,1,2,256,256]{5,4,3,2,1,0:T(8,128)} %param.6), kind=kLoop, calls=%fused_computation | loop fusion | flops 262144 | bytes 1572864 | tf_op jit(solution)/shard_map/transpose | solution.py:400
  3.4 0.8 copy.13
  4.2 64.7 %gather.1 = (f32[2,2,256,256]{3,2,1,0:T(8,128)}, f32[3,256]{1,0:T(4,128)}, f32[1,1]{1,0:T(1,128)}) custom-call(s32[12]{0:T(128)} %select_reduce_fusion.perm_ref, f32[24,128]{1,0:T(8,128)} %constant.9.clone.coef_ref, bf16[2,512,256]{2,1,0:T(8,128)(2,1)} %bitcast.12, bf16[12,2,2,256,256]{4,3,2,1,0:T(8,128)(2,1)} %bitcast.11), custom_call_target="tpu_custom_call" | custom-call | tf_op jit(solution)/shard_map/gather/pallas_call | solution.py:405
  68.9 0.0 copy-done
  68.9 0.0 copy-start.1
  68.9 1.2 %copy-done.1 = f32[2,2,256,256]{3,2,1,0:T(8,128)S(1)} copy-done((f32[2,2,256,256]{3,2,1,0:T(8,128)S(1)}, f32[2,2,256,256]{3,2,1,0:T(8,128)}, u32[]{:S(2)}) %copy-start.1) | copy-done | bytes 1048600
  70.2 10.3 %exponential.1 = f32[2,2,256,256]{3,2,1,0:T(8,128)} custom-call(f32[2,2,256,256]{3,2,1,0:T(8,128)S(1)} %copy-done.1, f32[2,2,256,256]{3,2,1,0:T(8,128)S(1)} %bitcast.10), custom_call_target="tpu_custom_call" | custom-call | tf_op jit(solution)/shard_map/exponential/pallas_call | solution.py:449
  80.5 1.3 %copy.17 = f32[3,256]{1,0:T(4,128)} copy(f32[3,256]{1,0:T(4,128)} %get-tuple-element.22) | data formatting | bytes 6144
Async XLA Ops:
  0.6 68.3 %copy-start = (f32[2,1,1,2,256,256]{5,4,3,2,1,0:T(8,128)S(1)}, f32[2,1,1,2,256,256]{5,4,3,2,1,0:T(8,128)}, u32[]{:S(2)}) copy-start(f32[2,1,1,2,256,256]{5,4,3,2,1,0:T(8,128)} %param.6) | copy-start | bytes 3145732
  68.9 1.2 %copy-start.1 = (f32[2,2,256,256]{3,2,1,0:T(8,128)S(1)}, f32[2,2,256,256]{3,2,1,0:T(8,128)}, u32[]{:S(2)}) copy-start(f32[2,2,256,256]{3,2,1,0:T(8,128)} %get-tuple-element.6.z_ref) | copy-start | bytes 3145732
where the time goes:
time: 83.8 us; the launch traced here: 83.5 us
  Pallas kernels  75 us (89%)
  local copies, waits for them, and re-layouts  3.32 us (4%)
  other arithmetic  2.77 us (3%)
  between operations  2.36 us (3%)
    pallas_call x1, Pallas kernels, per_device(): pl.pallas_call(functools.partial(gather_kernel, sizes, float(total_k)), o...  64.7 us
    pallas_call x1, Pallas kernels, per_device(): pl.pallas_call(exponential_kernel, grid=(depth,), out_shape=jax.ShapeDtyp...  10.3 us
    unnamed x5, local copies, waits for them, and re-layouts  2.49 us

commit v1 on v0

v1 whole, which is shorter than its diff:
```python
import functools
import math

import jax
import jax.numpy as jnp
import numpy as np
from jax import lax
from jax.experimental import pallas as pl
from jax.experimental.pallas import tpu as pltpu
from jax.sharding import PartitionSpec as P

TERMS = 12
MAGNITUDE_FLOOR = 0.25
DESCENT_STEP = 2.0
MESH = pl.DeviceIdType.MESH
AXES = ("kx", "ky", "kz")

DIRECTIONS = (
    [(sx, 0, sz) for sx in (-1, 1) for sz in (-1, 1)]
    + [(0, sy, sz) for sy in (-1, 1) for sz in (-1, 1)]
    + [(sx, sy, 0) for sx in (-1, 1) for sy in (-1, 1)]
)


def atan2(y, x):
    negative_y = (y < 0) | ((y == 0) & (1.0 / y < 0))
    negative_x = (x < 0) | ((x == 0) & (1.0 / x < 0))
    abs_y, abs_x = jnp.abs(y), jnp.abs(x)
    high, low = jnp.maximum(abs_y, abs_x), jnp.minimum(abs_y, abs_x)
    ratio = jnp.where(high == 0, 0.0, low / jnp.where(high == 0, 1.0, high))
    shifted = ratio > 0.4142135623730950
    t = jnp.where(shifted, (ratio - 1.0) / (ratio + 1.0), ratio)
    z = t * t
    poly = ((8.05374449538e-2 * z - 1.38776856032e-1) * z + 1.99777106478e-1) * z - 3.33329491539e-1
    angle = poly * z * t + t
    angle = jnp.where(shifted, angle + math.pi / 4, angle)
    angle = jnp.where(abs_y > abs_x, math.pi / 2 - angle, angle)
    angle = jnp.where(negative_x, math.pi - angle, angle)
    return jnp.where(negative_y, -angle, angle)


def split(value):
    high = value.astype(jnp.bfloat16)
    return high, (value - high.astype(jnp.float32)).astype(jnp.bfloat16)


def prepared(pair):
    return [split(part) for part in (pair[0], pair[1], pair[0] + pair[1])]


def product(left, right):
    real, imag, both = [
        jnp.dot(
            jnp.concatenate([a[0], a[0], a[1]], axis=1),
            jnp.concatenate([b[0], b[1], b[0]], axis=0),
            preferred_element_type=jnp.float32,
        )
        for a, b in zip(left, right)
    ]
    return real - imag, both - real - imag


def exponential_times(gauge, zr, zi):
    n = zr.shape[0]
    scale = 0.5 * DESCENT_STEP * 4.0
    x1 = (scale * (zr - zr.T), scale * (zi + zi.T))
    diagonal = lax.broadcasted_iota(jnp.int32, (n, n), 0) == lax.broadcasted_iota(
        jnp.int32, (n, n), 1
    )
    p1 = prepared(x1)
    x2 = product(p1, p1)
    p2 = prepared(x2)
    x3 = product(p1, p2)
    x4 = product(p2, p2)
    p4 = prepared(x4)
    inverse = [1.0 / math.factorial(k) for k in range(TERMS + 1)]

    def group(first, powers):
        real = jnp.where(diagonal, inverse[first], 0.0)
        imag = 0.0
        for k, power in enumerate(powers):
            real = real + inverse[first + 1 + k] * power[0]
            imag = imag + inverse[first + 1 + k] * power[1]
        return real, imag

    total = group(8, (x1, x2, x3, x4))
    for first in (4, 0):
        scaled = product(p4, prepared(total))
        base = group(first, (x1, x2, x3))
        total = (base[0] + scaled[0], base[1] + scaled[1])
    return product(prepared(gauge), prepared(total))


def step_kernel(
    sizes,
    total_k,
    offsets_ref,
    coef_ref,
    own_hbm,
    inter_hbm,
    gauge_hbm,
    out_ref,
    centres_ref,
    spread_ref,
    perm_ref,
    gauge_ref,
    z_ref,
    own_ref,
    inter_ref,
    basis_ref,
    left_ref,
    near_ref,
    end_ref,
    m_ref,
    dr_ref,
    di_ref,
    parts_ref,
    sums_near,
    sums_far,
    local_sem,
    send_sem,
    recv_sem,
    part_send,
    part_recv,
):
    depth, n = own_ref.shape[1], own_ref.shape[2]
    place = [lax.axis_index(axis) for axis in AXES]

    def moved(axis, by):
        return lax.rem(place[axis] + by + sizes[axis], sizes[axis])

    def step(axis, by):
        return {AXES[axis]: moved(axis, by)}

    plane = [
        (by, bz) for by in range(sizes[1]) for bz in range(sizes[2]) if by or bz
    ]

    own_copy = pltpu.make_async_copy(own_hbm, own_ref, local_sem.at[0])
    inter_copy = pltpu.make_async_copy(inter_hbm, inter_ref, local_sem.at[1])
    own_copy.start()
    inter_copy.start()
    gauge_copy = pltpu.make_async_copy(gauge_hbm, gauge_ref, local_sem.at[2])
    gauge_copy.start()

    barrier = pltpu.get_barrier_semaphore()
    for by, bz in plane:
        pl.semaphore_signal(
            barrier, inc=1, device_id={**step(1, by), **step(2, bz)}, device_id_type=MESH
        )
    for bx in range(1, sizes[0]):
        pl.semaphore_signal(barrier, inc=1, device_id=step(0, bx), device_id_type=MESH)
    pl.semaphore_wait(barrier, len(plane) + sizes[0] - 1)

    counter = [0]
    sent = []

    def send(source, target, device):
        index = counter[0]
        counter[0] += 1
        copy = pltpu.make_async_remote_copy(
            src_ref=source,
            dst_ref=target,
            send_sem=send_sem.at[index],
            recv_sem=recv_sem.at[index],
            device_id=device,
            device_id_type=MESH,
        )
        copy.start()
        sent.append(copy)
        return copy

    signs = (-1, 1)
    along_x, along_y, corner, rim = {}, {}, {}, {}
    for j in range(depth):
        for s, sign in enumerate(signs):
            along_x[s, j] = send(own_hbm.at[:, j], near_ref.at[s, 1 + j], step(0, -sign))
    odd = lax.rem(place[1], 2)
    ends = [
        send(own_hbm.at[:, depth - 1], end_ref.at[0], step(2, 1)),
        send(own_hbm.at[:, 0], end_ref.at[1], step(2, -1)),
    ]
    for j in reversed(range(depth)):
        for s, sign in enumerate(signs):
            along_y[s, j] = send(own_hbm.at[:, j], near_ref.at[2 + s, 1 + j], step(1, -sign))

    own_copy.wait()

    def make_basis(j, carry):
        real = own_ref[0, j].astype(jnp.float32).T
        imag = own_ref[1, j].astype(jnp.float32).T
        basis_ref[j, :n, :n] = real.astype(jnp.bfloat16)
        basis_ref[j, :n, n:] = imag.astype(jnp.bfloat16)
        basis_ref[j, n:, :n] = (-imag).astype(jnp.bfloat16)
        basis_ref[j, n:, n:] = real.astype(jnp.bfloat16)
        return carry

    lax.fori_loop(0, depth, make_basis, 0)
    codes = [
        offsets_ref[b, 0] * 9 + offsets_ref[b, 1] * 3 + offsets_ref[b, 2]
        for b in range(len(DIRECTIONS))
    ]
    for d, (ox, oy, oz) in enumerate(DIRECTIONS):
        found = jnp.int32(0)
        for b, code in enumerate(codes):
            found = found + jnp.where(code == ox * 9 + oy * 3 + oz, b, 0)
        perm_ref[d] = found
    inter_copy.wait()

    def make_left(q, carry):
        j = lax.rem(q, depth)
        b = perm_ref[q // depth]
        right = jnp.concatenate([inter_ref[b, 0, j], inter_ref[b, 1, j]], axis=0)
        left = jnp.dot(basis_ref[j], right, preferred_element_type=jnp.float32)
        left_ref[q] = left.astype(jnp.bfloat16)
        return carry

    lax.fori_loop(0, len(DIRECTIONS) * depth, make_left, 0)

    row_id = lax.broadcasted_iota(jnp.int32, (n, n), 0)
    col_id = lax.broadcasted_iota(jnp.int32, (n, n), 1)

    def multiply(direction, j, column, slot):
        q = direction * depth + j
        left = left_ref[q]
        real, imag = left[:n], left[n:]
        full = jnp.concatenate(
            [jnp.concatenate([real, -imag], axis=1), jnp.concatenate([imag, real], axis=1)], axis=0
        )
        m = jnp.dot(full, near_ref[column, slot].reshape(2 * n, n), preferred_element_type=jnp.float32)
        m_ref[q] = m
        diagonal = row_id == col_id
        dr_ref[pl.ds(q, 1), :] = jnp.sum(jnp.where(diagonal, m[:n], 0.0), axis=0, keepdims=True)
        di_ref[pl.ds(q, 1), :] = jnp.sum(jnp.where(diagonal, m[n:], 0.0), axis=0, keepdims=True)

    def inner_edges(first):
        count = 2 * (depth - 1)

        def body(i, carry):
            s = i // count
            r = lax.rem(i, count)
            up = r // (depth - 1)
            j = lax.rem(r, depth - 1) + 1 - up
            column = first + s
            multiply(2 * column + up, j, column, 1 + j + 2 * up - 1)
            return carry

        if count:
            lax.fori_loop(0, 2 * count, body, 0)

    def outer_edges(first, up):
        j = depth - 1 if up else 0

        def body(s, carry):
            column = first + s
            multiply(2 * column + up, j, column, 1 + j + 2 * up - 1)
            return carry

        lax.fori_loop(0, 2, body, 0)

    for j in reversed(range(depth)):
        for s in range(2):
            along_y[s, j].wait_recv()
        if j:
            for s, sign in enumerate(signs):
                corner[s, 0, j] = send(
                    near_ref.at[2 + odd, 1 + j], near_ref.at[4 + 2 * s + odd, 1 + j], step(0, -sign)
                )
    for up in range(2):
        ends[up].wait_recv()
        for s, sign in enumerate(signs):
            rim[1, s, up] = send(
                end_ref.at[up], near_ref.at[2 + s, (depth + 1) * up], step(1, -sign)
            )
    inner_edges(2)

    for j in range(depth):
        for s in range(2):
            along_x[s, j].wait_recv()
            source = near_ref.at[s, 1 + j]
            if j:
                corner[s, 1, j] = send(
                    source, near_ref.at[4 + 2 * s + odd, 1 + j], step(1, 1 - 2 * odd)
                )
            else:
                for other, sign in enumerate(signs):
                    corner[s, other, j] = send(
                        source, near_ref.at[4 + 2 * s + other, 1 + j], step(1, -sign)
                    )
            if j == depth - 1:
                rim[0, s, 0] = send(source, near_ref.at[s, 0], step(2, 1))
            if j == 0:
                rim[0, s, 1] = send(source, near_ref.at[s, depth + 1], step(2, -1))
    inner_edges(0)

    for up in range(2):
        for s in range(2):
            rim[1, s, up].wait_recv()
        outer_edges(2, up)

    for j in range(depth):
        for s in range(2):
            for other in range(2):
                corner[s, other, j].wait_recv()

        def corners(c, carry, j=j):
            multiply(8 + c, j, 4 + c, 1 + j)
            return carry

        lax.fori_loop(0, 4, corners, 0)

    for up in (1, 0):
        for s in range(2):
            rim[0, s, up].wait_recv()
        outer_edges(0, up)

    dr, di = dr_ref[...], di_ref[...]
    phase = atan2(di, dr)
    squared = dr * dr + di * di
    coef = coef_ref[...]
    weight = coef[:, 0:1]
    weighted = weight * phase
    parts = [
        jnp.sum(coef[:, 1 + a : 2 + a] * weighted, axis=0, keepdims=True) for a in range(3)
    ]
    parts.append(
        jnp.sum(weight * (1.0 - squared + phase * phase), axis=0, keepdims=True)
    )
    parts.append(jnp.zeros((4, n), jnp.float32))
    value = jnp.concatenate(parts, axis=0)
    index = 0
    for stage, slots in enumerate((sums_near, sums_far)):
        if stage == 0:
            me = place[1] * sizes[2] + place[2]
            others = [
                (
                    {**step(1, by), **step(2, bz)},
                    moved(1, -by) * sizes[2] + moved(2, -bz),
                )
                for by, bz in plane
            ]
        else:
            me = place[0]
            others = [(step(0, bx), moved(0, -bx)) for bx in range(1, sizes[0])]
        parts_ref[stage] = value
        slots[me] = value
        arrivals = []
        for device, source in others:
            copies = [
                pltpu.make_async_remote_copy(
                    src_ref=parts_ref.at[stage],
                    dst_ref=slots.at[slot],
                    send_sem=part_send.at[index],
                    recv_sem=part_recv.at[index],
                    device_id=device,
                    device_id_type=MESH,
                )
                for slot in (me, source)
            ]
            copies[0].start()
            sent.append(copies[0])
            arrivals.append(copies[1])
            index += 1
        for copy in arrivals:
            copy.wait_recv()
        value = slots[0]
        for other in range(1, len(others) + 1):
            value = value + slots[other]

    centres = -value[0:3] / total_k
    centres_ref[...] = centres
    per_band = value[3:4] / total_k - jnp.sum(centres * centres, axis=0, keepdims=True)
    spread_ref[...] = jnp.sum(per_band, axis=1, keepdims=True)

    angle = phase
    for a in range(3):
        angle = angle + coef[:, 1 + a : 2 + a] * centres[a : a + 1]
    angle = angle / jnp.maximum(squared, MAGNITUDE_FLOOR)
    dr_ref[...] = weight * (dr + di * angle)
    di_ref[...] = weight * (dr * angle - di)

    strip = 32

    def combine(i, carry):
        j = i // (n // strip)
        start = pl.multiple_of(lax.rem(i, n // strip) * strip, strip)
        real = jnp.zeros((strip, n), jnp.float32)
        imag = jnp.zeros((strip, n), jnp.float32)
        for d in range(len(DIRECTIONS)):
            q = d * depth + j
            cr = dr_ref[pl.ds(q, 1), :]
            ci = di_ref[pl.ds(q, 1), :]
            mr = m_ref[q, pl.ds(start, strip), :]
            mi = m_ref[q, pl.ds(n + start, strip), :]
            real = real + (mr * cr - mi * ci)
            imag = imag + (mr * ci + mi * cr)
        z_ref[j, 0, pl.ds(start, strip), :] = real
        z_ref[j, 1, pl.ds(start, strip), :] = imag
        return carry

    lax.fori_loop(0, depth * (n // strip), combine, 0)

    gauge_copy.wait()

    def update(j, carry):
        new = exponential_times(
            (gauge_ref[0, j], gauge_ref[1, j]), z_ref[j, 0], z_ref[j, 1]
        )
        out_ref[0, j] = new[0]
        out_ref[1, j] = new[1]
        return carry

    lax.fori_loop(0, depth, update, 0)
    for copy in sent:
        copy.wait_send()


def per_device(sizes, offsets, gauge, intersections):
    depth, n = gauge.shape[3], gauge.shape[4]
    counts = (sizes[0], sizes[1], sizes[2] * depth)
    total_k = counts[0] * counts[1] * counts[2]
    table = np.array(DIRECTIONS, np.float64)
    bvec = table * (2.0 * math.pi / np.array(counts, np.float64))
    weight = 1.0 / (4.0 * np.sum(bvec * bvec, axis=1))
    queue = len(DIRECTIONS) * depth
    coef = np.zeros((queue, 128), np.float32)
    coef[:, 0] = np.repeat(weight, depth)
    coef[:, 1:4] = np.repeat(bvec, depth, axis=0)
    flat = gauge.reshape(2, depth, n, n)
    own = flat.astype(jnp.bfloat16)
    inter = intersections.reshape(len(DIRECTIONS), 2, depth, n, n)
    copies = 8 * depth + 10
    bf16, f32 = jnp.bfloat16, jnp.float32
    near = sizes[1] * sizes[2]
    partners = near + sizes[0] - 2
    updated, centres, spread = pl.pallas_call(
        functools.partial(step_kernel, sizes, float(total_k)),
        out_shape=(
            jax.ShapeDtypeStruct((2, depth, n, n), f32),
            jax.ShapeDtypeStruct((3, n), f32),
            jax.ShapeDtypeStruct((1, 1), f32),
        ),
        in_specs=[
            pl.BlockSpec(memory_space=pltpu.SMEM),
            pl.BlockSpec(memory_space=pltpu.VMEM),
            pl.BlockSpec(memory_space=pl.ANY),
            pl.BlockSpec(memory_space=pl.ANY),
            pl.BlockSpec(memory_space=pl.ANY),
        ],
        out_specs=(
            pl.BlockSpec(memory_space=pltpu.VMEM),
            pl.BlockSpec(memory_space=pltpu.VMEM),
            pl.BlockSpec(memory_space=pltpu.VMEM),
        ),
        scratch_shapes=[
            pltpu.SMEM((len(DIRECTIONS),), jnp.int32),
            pltpu.VMEM((2, depth, n, n), f32),
            pltpu.VMEM((depth, 2, n, n), f32),
            pltpu.VMEM((2, depth, n, n), bf16),
            pltpu.VMEM(inter.shape, bf16),
            pltpu.VMEM((depth, 2 * n, 2 * n), bf16),
            pltpu.VMEM((queue, 2 * n, n), bf16),
            pltpu.VMEM((8, depth + 2, 2, n, n), bf16),
            pltpu.VMEM((2, 2, n, n), bf16),
            pltpu.VMEM((queue, 2 * n, n), f32),
            pltpu.VMEM((queue, n), f32),
            pltpu.VMEM((queue, n), f32),
            pltpu.VMEM((2, 8, n), f32),
            pltpu.VMEM((near, 8, n), f32),
            pltpu.VMEM((sizes[0], 8, n), f32),
            pltpu.SemaphoreType.DMA((3,)),
            pltpu.SemaphoreType.DMA((copies,)),
            pltpu.SemaphoreType.DMA((copies,)),
            pltpu.SemaphoreType.DMA((partners,)),
            pltpu.SemaphoreType.DMA((partners,)),
        ],
        compiler_params=pltpu.CompilerParams(
            collective_id=0, has_side_effects=True, vmem_limit_bytes=58 * 1024 * 1024
        ),
        name="step",
    )(offsets, jnp.asarray(coef), own, inter, flat)
    return updated.reshape(2, 1, 1, depth, n, n), centres, spread.reshape(())


def solution(mesh):
    sizes = tuple(mesh.shape[axis] for axis in AXES)
    return jax.shard_map(
        functools.partial(per_device, sizes),
        mesh=mesh,
        in_specs=(
            P(),
            P(None, "kx", "ky", "kz", None, None),
            P(None, None, "kx", "ky", "kz", None, None),
        ),
        out_specs=(P(None, "kx", "ky", "kz", None, None), P(), P()),
        check_vma=False,
    )
```

time: 83.8 us -> 73.9 us (0.88)
  Pallas kernels: 75 us -> 64.2 us
  local copies, waits for them, and re-layouts: 3.32 us -> 4.91 us
    pallas_call x2 -> x1, Pallas kernels: 75 us -> 64.2 us  [per_device(): pl.pallas_call(functools.partial(step_kernel, sizes, float(total_k)), out...]
    unnamed x5 -> x3, local copies, waits for them, and re-layouts: 2.49 us -> 4.91 us
    convert_element_type x0 -> x1, other arithmetic: none -> 2.07 us  [per_device(): own = flat.astype(jnp.bfloat16)]
    transpose x1 -> x0, other arithmetic: 1.28 us -> none  [per_device(): own = jnp.swapaxes(flat.astype(jnp.bfloat16), 0, 1).reshape(depth, 2 * n, n)]
    reduce_and x1 -> x0, other arithmetic: 0.87 us -> none  [per_device(): same = jnp.all(canonical[:, None, :] == offsets[None, :, :], axis=2)]
where the time goes in v1:
time: 73.9 us; the launch traced here: 73.6 us
  Pallas kernels  64.2 us (87%)
  local copies, waits for them, and re-layouts  4.91 us (7%)
  between operations  2.4 us (3%)
  other arithmetic  2.07 us (3%)
    pallas_call x1, Pallas kernels, per_device(): pl.pallas_call(functools.partial(step_kernel, sizes, float(total_k)), out...  64.2 us
    unnamed x3, local copies, waits for them, and re-layouts  4.91 us
    convert_element_type x1, other arithmetic, per_device(): own = flat.astype(jnp.bfloat16)  2.07 us

profile of v1, /device:TPU:0, one launch (start us, length us, event | category | flops | bytes accessed | tf_op | source)
XLA Modules:
  0.0 73.6 jit_solution(6263761193777859270)
XLA Ops:
  0.6 1.4 %copy.7.offsets_ref = s32[12,3]{1,0:T(8,128)} copy(s32[12,3]{0,1:T(4,128)} %param.4) | data formatting | bytes 288 | tf_op args[0]
  2.0 2.1 %bitcast_convert_fusion.own_hbm = bf16[2,2,256,256]{3,2,1,0:T(8,128)(2,1)} fusion(f32[2,1,1,2,256,256]{5,4,3,2,1,0:T(8,128)} %param.5), kind=kLoop, calls=%fused_computation | loop fusion | flops 262144 | bytes 1572864 | tf_op jit(solution)/shard_map/convert_element_type | solution.py:430
  4.1 64.2 %step.1 = (f32[2,2,256,256]{3,2,1,0:T(8,128)}, f32[3,256]{1,0:T(4,128)}, f32[1,1]{1,0:T(1,128)}) custom-call(s32[12,3]{1,0:T(8,128)} %copy.7.offsets_ref, f32[24,128]{1,0:T(8,128)} %constant.2.clone.coef_ref, bf16[2,2,256,256]{3,2,1,0:T(8,128)(2,1)} %bitcast_convert_fusion.own_hbm, bf16[12,2,2,256,256]{4,3,2,1,0:T(8,128)(2,1)} %bitcast.7, ...), custom_call_target="tpu_custom_call" | custom-call | tf_op jit(solution)/shard_map/step/pallas_call | solution.py:436
  68.3 2.3 %copy.12 = f32[2,1,1,2,256,256]{5,4,3,2,1,0:T(8,128)} copy(f32[2,1,1,2,256,256]{5,4,3,2,1,0:T(8,128)} %bitcast.9) | data formatting | bytes 2097152
  70.6 1.3 %copy.13 = f32[3,256]{1,0:T(4,128)} copy(f32[3,256]{1,0:T(4,128)} %get-tuple-element.16) | data formatting | bytes 6144
